TPU v7x, 128 devices: a whole 4x4x4 slice. The times are simulated.
128 devices in a mesh: row: 32 (over z, x, core), col: 4 (over y).
Axes of the slice: x: 4, y: 4, z: 4, core: 2. Of those that a mesh axis runs over, the one named last changes fastest.
Arguments:
- spikes: int32 [10, 16384], P(None, ('row', 'col')), may hold values 0 or 1
- stp_init: float32 [2, 16384], P(None, ('row', 'col')), may hold values from 0.2 to 1
- trace_init: float32 [3, 16384], P(None, ('row', 'col')), may hold values from 0 to 1.5
- weights: float32 [32, 4, 256, 128, 128], P('row', 'col'), may hold values from 0 to 1
- block_pre: int32 [32, 4, 256], P('row', 'col'), may hold values from 0 to 31
- block_post: int32 [32, 4, 256], P('row', 'col'), may hold values from 0 to 3
- block_count: int32 [32, 4], P('row', 'col'), may hold values from 1 to 255, as said below
Outputs:
- new_weights: float32 [32, 4, 128, 128, 128], P('row', 'col')
- synaptic: float32 [10, 16384], P(None, ('row', 'col'))
Inputs may be any that keep to these rules, and one draw needn't show every extreme that they name: block_count[r, c] + block_count[(r + 16) mod 32, c] = 256; some device uses 2 * 128 - 1 slots in every draw.
All inputs are finite; a program needn't handle non-finite values. No bound on the sum of `spikes` on one device may be relied on, other than what follows from the above.
Results may differ from a plain program's by a relative error of at most 0.0003.
Values sent between devices are 32-bit elements; how exact they have to be, the bound alone decides.
A program may use at most 128 MiB of HBM per device.

v0:
```python
import functools
import math

import jax
import jax.numpy as jnp
from jax import lax
from jax.experimental import pallas as pl
from jax.experimental.pallas import tpu as pltpu
from jax.sharding import PartitionSpec as P

BASE_USE = 0.25
USE_DECAY = 0.98
SUPPLY_RATE = 0.005
PLUS_DECAY = math.exp(-1.0 / 16.8)
MINUS_DECAY = math.exp(-1.0 / 33.7)
SLOW_DECAY = math.exp(-1.0 / 114.0)
SYN_DECAY = math.exp(-1.0 / 5.0)
PAIR_UP = 1.0
TRIPLET_UP = 0.8
PAIR_DOWN = 0.9
LEARN_RATE = 0.02
WEIGHT_MAX = 1.0
INHIB_GAIN = 4.0

G = 128
HALF = 128
STEPS = 10
ROWS = 32
COLS = 4
MESH = pl.DeviceIdType.MESH
F32 = jnp.float32
I32 = jnp.int32
BF16 = jnp.bfloat16

EA = 4
EB = 3
ES = 32
M0 = 16
RUNGS = ((16, 22, 28, 30), (16, 23, 29, 32), (17, 25, 31, 35), (20, 32, 40, 44))
M0_FIRST = 6
ITERS = 12
STEP_W = 10.0
INVERSE = (0, 3, 4, 1, 2, 7, 8, 5, 6)
RANGES = tuple(
    [(k, EA, (k - 1) * EA) for k in range(1, 9)]
    + [(k, EB, 8 * EA + (k - 1) * EB) for k in range(1, 9)]
    + [(0, ES, 8 * (EA + EB))]
)
BACK = tuple([INVERSE[k] - 1 for k in range(1, 9)] + [7 + INVERSE[k] for k in range(1, 9)] + [16])
SPREAD = 8 * (EA + EB) + ES
VMEM_LIMIT = 60 * 1024 * 1024
ANY = pl.BlockSpec(memory_space=pl.ANY)
SMEM = pl.BlockSpec(memory_space=pltpu.SMEM)
VMEM = pl.BlockSpec(memory_space=pltpu.VMEM)


def place():
    row, col = lax.axis_index("row"), lax.axis_index("col")
    return row, col


def at(row, col):
    return {"row": row, "col": col}


def flip_core(row):
    return row + 1 - 2 * lax.rem(row, 2)


def across(row):
    return lax.rem(row + ROWS // 2, ROWS)


def shift_x(row, step):
    within = lax.rem(row, 8)
    return row - within + lax.rem(within + 2 * step + 8, 8)


def neighbour(k, row, col):
    if k == 0:
        return at(flip_core(row), col)
    which, other = (k - 1) // 2, (k - 1) % 2
    if which < 2:
        row = shift_x(row, 1 if which == 0 else -1)
    else:
        col = lax.rem(col + (1 if which == 2 else COLS - 1), COLS)
    return at(flip_core(row) if other else row, col)


def greet(peers):
    barrier = pltpu.get_barrier_semaphore()
    for peer in peers:
        pl.semaphore_signal(barrier, inc=1, device_id=peer, device_id_type=MESH)
    pl.semaphore_wait(barrier, len(peers))


def send(src, dst, send_sem, recv_sem, peer):
    return pltpu.make_async_remote_copy(
        src_ref=src, dst_ref=dst, send_sem=send_sem, recv_sem=recv_sem, device_id=peer, device_id_type=MESH
    )


def first_kernel(
    spikes, stp, trace, held, pre, post, weights,
    tab, rtab, ptab, pidx, tables, rung, z0, early,
    pack, idx, cnt, s1, r1, s2, r2, s3, r3, s4, r4, s5, r5, s6, r6, s7, r7, s8, r8,
):
    row, col = place()
    far = across(row)
    mate = at(far, col)
    barrier = pltpu.get_barrier_semaphore()

    plane, within = row // 8, lax.rem(row, 8)

    def in_plane(d):
        return plane * 8 + lax.rem(within + d, 8)

    for d in range(1, 8):
        pl.semaphore_signal(barrier, inc=1, device_id=at(in_plane(d), col), device_id_type=MESH)
    for d in range(1, 4):
        pl.semaphore_signal(barrier, inc=1, device_id=at(lax.rem(row + 8 * d, ROWS), col), device_id_type=MESH)
    for d in range(1, COLS):
        c = lax.rem(col + d, COLS)
        pl.semaphore_signal(barrier, inc=1, device_id=at(row, c), device_id_type=MESH)
        pl.semaphore_signal(barrier, inc=1, device_id=at(far, c), device_id_type=MESH)
    for k in (6, 8):
        pl.semaphore_signal(barrier, inc=1, device_id=neighbour(k, row, col), device_id_type=MESH)

    count_row = jnp.broadcast_to(held[...].astype(F32), (1, G))
    pack[pl.ds(0, STEPS), :] = spikes[...].astype(F32)
    pack[pl.ds(10, 2), :] = stp[...]
    pack[pl.ds(12, 3), :] = trace[...]
    pack[pl.ds(15, 1), :] = count_row
    idx[...] = jnp.concatenate([pre[pl.ds(1, 1), :], post[pl.ds(1, 1), :], jnp.zeros((6, G), I32)], axis=0)
    cnt[row, col] = count_row
    tab[row] = pack[...]
    rtab[col] = pack[...]
    pl.semaphore_wait(barrier, 7 + 3 + 2 * (COLS - 1) + 2)

    for d in range(1, COLS):
        c = lax.rem(col + d, COLS)
        send(cnt.at[row, col], cnt.at[row, col], s4.at[d], r4.at[1 + col], at(row, c)).start()
    z_parts = [
        send(weights.at[pl.ds(HALF + a, n)], z0.at[pl.ds(a, n)], s6.at[17 + i], r6.at[17 + i], mate)
        for i, (a, n) in enumerate(((0, M0_FIRST), (M0_FIRST, M0 - M0_FIRST)))
    ]
    z_parts[0].start()
    ahead = []
    for i, (k, n, base) in enumerate(RANGES):
        there = RANGES[BACK[i]][2]
        ahead.append(
            send(
                weights.at[pl.ds(HALF + M0 + base, n)], early.at[pl.ds(there, n)],
                s6.at[i], r6.at[BACK[i]], neighbour(k, row, col),
            )
        )
    along_y = [copy for copy, (k, _, _) in zip(ahead, RANGES) if k > 4]
    others = [copy for copy, (k, _, _) in zip(ahead, RANGES) if k <= 4]
    for d in range(1, COLS):
        c = lax.rem(col + d, COLS)
        send(pack, rtab.at[col], s2.at[d], r2.at[col], at(row, c)).start()
    for copy in along_y:
        copy.start()
    for d in range(1, COLS):
        c = lax.rem(col + d, COLS)
        send(cnt.at[row, c], cnt.at[row, c], s4.at[d], r4.at[1 + c], at(row, c)).wait()

    for d in range(1, 8):
        send(cnt.at[row], cnt.at[row], s5.at[d], r5.at[within], at(in_plane(d), col)).start()
    for d in range(1, 8):
        send(pack, tab.at[row], s1.at[d], r1.at[within], at(in_plane(d), col)).start()
    for copy in others:
        copy.start()
    for d in range(1, 8):
        source = in_plane(d)
        send(cnt.at[source], cnt.at[source], s5.at[d], r5.at[lax.rem(within + d, 8)], at(source, col)).wait()
    ours = pl.ds(plane * 8, 8)
    for d in range(1, 4):
        peer = at(lax.rem(row + 8 * d, ROWS), col)
        send(cnt.at[ours], cnt.at[ours], s7.at[d], r7.at[plane], peer).start()
    for d in range(COLS):
        c = lax.rem(col + d, COLS)
        send(pack, ptab.at[col], s3.at[d], r3.at[col], at(far, c)).start()
    last = send(idx, pidx, s4.at[0], r4.at[0], mate)
    last.start()
    for d in range(1, 8):
        source = in_plane(d)
        send(pack, tab.at[source], s1.at[d], r1.at[lax.rem(within + d, 8)], at(source, col)).wait()
    for d in range(1, 4):
        peer = at(lax.rem(row + 8 * d, ROWS), col)
        send(tab.at[ours], tab.at[ours], s8.at[d], r8.at[plane], peer).start()
    z_parts[1].start()
    for d in range(1, 4):
        p = lax.rem(plane + d, 4)
        theirs = pl.ds(p * 8, 8)
        send(cnt.at[theirs], cnt.at[theirs], s7.at[d], r7.at[p], at(lax.rem(row + 8 * d, ROWS), col)).wait()

    make_plan(row, col, cnt, tables, rung)

    for d in range(1, 4):
        p = lax.rem(plane + d, 4)
        theirs = pl.ds(p * 8, 8)
        send(tab.at[theirs], tab.at[theirs], s8.at[d], r8.at[p], at(lax.rem(row + 8 * d, ROWS), col)).wait()
    for d in range(1, COLS):
        c = lax.rem(col + d, COLS)
        send(pack, rtab.at[c], s2.at[d], r2.at[c], at(row, c)).wait()
    for d in range(COLS):
        c = lax.rem(col + d, COLS)
        send(pack, ptab.at[c], s3.at[d], r3.at[c], at(far, c)).wait()
    last.wait()
    for part in z_parts:
        part.wait()
    for i, (k, n, base) in enumerate(RANGES):
        send(
            weights.at[pl.ds(HALF + M0 + base, n)], early.at[pl.ds(base, n)], s6.at[i], r6.at[i], neighbour(k, row, col)
        ).wait()


def first(spikes, stp, trace, held, pre, post, weights):
    dma = pltpu.SemaphoreType.DMA
    return pl.pallas_call(
        first_kernel,
        out_shape=(
            jax.ShapeDtypeStruct((ROWS, 16, G), F32),
            jax.ShapeDtypeStruct((COLS, 16, G), F32),
            jax.ShapeDtypeStruct((COLS, 16, G), F32),
            jax.ShapeDtypeStruct((8, G), I32),
            jax.ShapeDtypeStruct((8, G), I32),
            jax.ShapeDtypeStruct((1,), I32),
            jax.ShapeDtypeStruct((M0, G, G), F32),
            jax.ShapeDtypeStruct((SPREAD, G, G), F32),
        ),
        in_specs=[VMEM] * 6 + [ANY],
        out_specs=(VMEM, VMEM, VMEM, VMEM, VMEM, SMEM, ANY, ANY),
        scratch_shapes=[
            pltpu.VMEM((16, G), F32), pltpu.VMEM((8, G), I32),
            pltpu.VMEM((ROWS, COLS, 1, G), F32),
            dma((8,)), dma((8,)), dma((COLS,)), dma((COLS,)), dma((COLS,)), dma((COLS,)),
            dma((COLS,)), dma((COLS + 1,)), dma((8,)), dma((8,)), dma((19,)), dma((19,)),
            dma((4,)), dma((4,)), dma((4,)), dma((4,)),
        ],
        compiler_params=pltpu.CompilerParams(
            collective_id=0, has_side_effects=True, vmem_limit_bytes=VMEM_LIMIT
        ),
        name="first",
    )(spikes, stp, trace, held, pre, post, weights)


def make_plan(row, col, cnt, tables, rung):
    shape = (8, G)
    lane = lax.broadcasted_iota(I32, shape, 1)
    slot = lax.broadcasted_iota(I32, (1, G), 1)

    def pick(r, total):
        for c in range(COLS):
            total = jnp.where(slot == c * ROWS + r, cnt[r, c], total)
        return total

    total = lax.fori_loop(0, ROWS, pick, jnp.zeros((1, G), F32))
    count = jnp.broadcast_to(total, shape)
    surplus = jnp.maximum(count - HALF, 0.0)
    core = lax.rem(lane, 2)
    x_at = lax.rem(lane, 8) // 2
    z_hi = lax.rem(lane, 32) // 16

    def roll(value, by):
        return pltpu.roll(value, by % G, 1)

    def from_sibling(v):
        return jnp.where(core == 0, roll(v, -1), roll(v, 1))

    def seen(v):
        same = (
            jnp.where(x_at == 3, roll(v, 6), roll(v, -2)),
            jnp.where(x_at == 0, roll(v, -6), roll(v, 2)),
            roll(v, -ROWS),
            roll(v, ROWS),
        )
        out = [from_sibling(v)]
        for value in same:
            out += [value, from_sibling(value)]
        return out

    def toward(which, v):
        if which == 0:
            return jnp.where(x_at == 3, roll(v, 6), roll(v, -2))
        if which == 1:
            return jnp.where(x_at == 0, roll(v, -6), roll(v, 2))
        return roll(v, -ROWS if which == 2 else ROWS)

    def arriving(v):
        out = [from_sibling(v[0])]
        for k in range(1, 9):
            value = toward((k - 1) // 2, v[INVERSE[k]])
            out.append(from_sibling(value) if (k - 1) % 2 else value)
        return out

    def add(values):
        return functools.reduce(jnp.add, values)

    zero = jnp.zeros(shape, F32)
    free = jnp.maximum(surplus - M0, 0.0)
    tops = [jnp.clip(surplus - float(M0 + base), 0.0, float(n)) for _, n, base in RANGES]
    top_a = [zero] + tops[:8]
    top = [tops[16]] + [tops[i] + tops[8 + i] for i in range(8)]
    outs, ins = [zero] * 9, [zero] * 9
    for _ in range(ITERS):
        load = jnp.maximum(surplus - add(outs), float(M0)) + add(ins)
        near = seen(load)
        outs = [jnp.clip(outs[k] + (load - near[k]) * (1.0 / STEP_W), 0.0, top[k]) for k in range(9)]
        scale = jnp.minimum(1.0, free / jnp.maximum(add(outs), 1e-6))
        outs = [v * scale for v in outs]
        ins = arriving(outs)
    give = [jnp.minimum(jnp.floor(v + 0.5), top[k]) for k, v in enumerate(outs)]
    over = jnp.maximum(add(give) - free, 0.0)
    for k in range(9):
        less = jnp.minimum(give[k], over)
        give[k] = give[k] - less
        over = over - less
    give_a = [jnp.minimum(give[k], top_a[k]) for k in range(9)]
    give_b = [give[k] - give_a[k] for k in range(9)]
    take_a, take_b = arriving(give_a), arriving(give_b)
    gives = give_a[1:] + give_b[1:] + give_b[:1]
    takes = take_a[1:] + take_b[1:] + take_b[:1]
    lefts = [tops[i] - gives[i] for i in range(17)]
    in_a = add(takes[:8])
    in_ab = in_a + add(takes[8:16])
    in_all = in_ab + takes[16]
    most = [jnp.max(v) for v in (in_a, in_ab, in_all, in_all + free - add(give))]
    picked = jnp.int32(len(RUNGS))
    for i in reversed(range(len(RUNGS))):
        fits = functools.reduce(jnp.logical_and, [m <= float(n) for m, n in zip(most, RUNGS[i])])
        picked = jnp.where(fits, i, picked)
    full = picked == len(RUNGS)
    rung[0] = picked

    me = col * ROWS + row
    mate = col * ROWS + across(row)

    def of(v, who):
        return jnp.max(jnp.where(lane == who, v, -1.0), axis=1, keepdims=True).astype(I32)[:1]

    def table(i, value, most):
        tables[pl.ds(i, 1), :] = jnp.clip(value, 0, most)

    none = jnp.zeros((1, 1), I32)
    held = of(count, me)
    give_me = [of(v, me) for v in gives]
    left_me = [of(v, me) for v in lefts]
    in_me = of(in_all, me)
    r = slot - in_me
    j = M0 + SPREAD + r - add(left_me)
    before = none
    for i, (_, _, base) in enumerate(RANGES):
        here = (r >= before) & (r < before + left_me[i])
        j = jnp.where(here, M0 + base + give_me[i] + r - before, j)
        before = before + left_me[i]
    table(1, j, HALF - 1)
    source = jnp.zeros((1, G), I32)
    kind = jnp.zeros((1, G), I32)
    gather = jnp.zeros((1, G), I32)
    before, ahead = none, none
    for i, (_, n, base) in enumerate(RANGES):
        amount = of(takes[i], me)
        here = (slot >= before) & (slot < before + amount)
        source = jnp.where(here, base + slot - before, source)
        kind = jnp.where(here, 1, kind)
        before = before + amount
        here = (slot >= base) & (slot < base + n)
        gather = jnp.where(here, slot - base + ahead, gather)
        ahead = ahead + of(takes[i], mate)
    table(2, source, SPREAD - 1)
    table(3, kind, 1)
    table(4, gather, HALF - 1)
    table(0, slot, HALF - 1)
    j = slot - held
    left = none
    r = jnp.zeros((1, G), I32)
    passed = jnp.zeros((1, G), I32)
    for i, (_, n, base) in enumerate(RANGES):
        amount = of(gives[i], mate)
        inside = j - (M0 + base)
        here = (inside >= 0) & (inside < n)
        passed = jnp.where(here & (inside < amount), 1, passed)
        r = jnp.where(here, left + inside - amount, r)
        left = left + of(lefts[i], mate)
    r = jnp.where(j >= M0 + SPREAD, left + j - (M0 + SPREAD), r)
    spot = jnp.where(passed == 1, HALF + j - M0, of(in_all, mate) + r)
    spot = jnp.where(full, j, spot)
    kind = jnp.where(j < 0, 0, jnp.where((j < M0) & jnp.logical_not(full), 2, 1))
    spot = jnp.where(kind == 2, j, spot)
    table(5, spot, HALF + SPREAD - 1)
    table(6, kind, 2)
    table(7, j, HALF - 1)


def move_kernel(ends, tables, weights, early, staged, up, held, back, *rest):
    outs, gots = rest[:4], rest[4:8]
    ls, zs, zr, gs, gr = rest[8:]
    starts = (0,) + ends[:3]
    row, col = place()
    mate = at(across(row), col)
    peers = [neighbour(k, row, col) for k in range(9)]
    load = pltpu.make_async_copy(weights.at[pl.ds(HALF, HALF)], up, ls.at[0])
    load.start()
    load_early = pltpu.make_async_copy(early, held, ls.at[1])
    load_early.start()
    greet(peers + [mate])
    load_early.wait()
    load.wait()
    zs_all = [send(outs[i], gots[i], zs.at[i], zr.at[i], mate) for i in range(4)]
    for part in range(4):
        start, target = starts[part], outs[part]

        @pl.loop(0, ends[part] - start)
        def _(i):
            t = start + i
            target[i] = jnp.where(tables[3, t] == 1, held[tables[2, t]], up[tables[1, t]])

        zs_all[part].start()

    def received(t, parts):
        value = gots[0][jnp.minimum(t, ends[0] - 1)]
        for p in range(1, parts):
            size = ends[p] - starts[p]
            value = jnp.where(t < starts[p], value, gots[p][jnp.clip(t - starts[p], 0, size - 1)])
        return value

    waits, stores = [], []
    for part in range(4):
        zs_all[part].wait_recv()
        for i, (k, n, base) in enumerate(RANGES):
            if i // 8 != part:
                continue

            @pl.loop(base, base + n)
            def _(slot):
                back[slot] = received(tables[4, slot], part + 1)

            there = RANGES[BACK[i]][2]
            send(
                back.at[pl.ds(base, n)], staged.at[pl.ds(HALF + there, n)], gs.at[i], gr.at[BACK[i]], peers[k]
            ).start()
            waits.append(send(back.at[pl.ds(base, n)], staged.at[pl.ds(HALF + base, n)], gs.at[i], gr.at[i], peers[k]))
        store = pltpu.make_async_copy(
            gots[part], staged.at[pl.ds(starts[part], ends[part] - starts[part])], ls.at[2 + part]
        )
        store.start()
        stores.append(store)
    for store in stores:
        store.wait()
    for copy in zs_all:
        copy.wait_send()
    for come in waits:
        come.wait()


def full_kernel(weights, staged, ss, rs):
    row, col = place()
    mate = at(across(row), col)
    greet([mate])
    copy = send(weights.at[pl.ds(HALF, HALF)], staged.at[pl.ds(0, HALF)], ss, rs, mate)
    copy.start()
    copy.wait()


STAGED = jax.ShapeDtypeStruct((HALF + SPREAD, G, G), F32)


def move(index, tables, weights, early):
    dma = pltpu.SemaphoreType.DMA
    if index == len(RUNGS):
        return pl.pallas_call(
            full_kernel,
            out_shape=STAGED,
            in_specs=[ANY],
            out_specs=ANY,
            scratch_shapes=[dma, dma],
            compiler_params=pltpu.CompilerParams(
                collective_id=2 + index, has_side_effects=True, vmem_limit_bytes=VMEM_LIMIT
            ),
            name="move_full",
        )(weights)
    ends = RUNGS[index]

    def blocks(n):
        return pltpu.VMEM((n, G, G), F32)

    parts = [blocks(b - a) for a, b in zip((0,) + ends[:3], ends)]
    return pl.pallas_call(
        functools.partial(move_kernel, ends),
        out_shape=STAGED,
        in_specs=[SMEM, ANY, ANY],
        out_specs=ANY,
        scratch_shapes=[
            blocks(HALF), blocks(SPREAD), blocks(SPREAD), *parts, *parts,
            dma((6,)), dma((4,)), dma((4,)), dma((17,)), dma((17,)),
        ],
        compiler_params=pltpu.CompilerParams(
            collective_id=2 + index, has_side_effects=True, vmem_limit_bytes=VMEM_LIMIT
        ),
        name=f"move_{ends[3]}",
    )(tables, weights, early)


CHUNK = 8
KP = 64


def split(value):
    high = value.astype(BF16)
    return high, (value - high.astype(F32)).astype(BF16)


def blocks_kernel(
    tables, pre, post, pidx, tab, rtab, ptab, weights, staged, z0, new, cur, qs, ds, ps, scr, acc, win, wout, sem_in, sem_out
):
    steps = HALF // CHUNK

    @pl.loop(0, HALF, unroll=4)
    def _(s):
        kind, spot, arrived = tables[6, s], tables[5, s], sem_in.at[s // CHUNK]

        @pl.when(kind == 0)
        def _():
            pltpu.make_async_copy(weights.at[s], win.at[s], arrived).start()

        @pl.when(kind == 1)
        def _():
            pltpu.make_async_copy(staged.at[spot], win.at[s], arrived).start()

        @pl.when(kind == 2)
        def _():
            pltpu.make_async_copy(z0.at[jnp.minimum(spot, M0 - 1)], win.at[s], arrived).start()

    neuron = lax.broadcasted_iota(I32, (1, G), 1)
    lane = lax.broadcasted_iota(I32, (G, G), 1)
    polarity = jnp.where(lax.rem(neuron, 5) == 4, -INHIB_GAIN, 1.0).astype(F32)

    use, supply, fast = tab[:, 10, :], tab[:, 11, :], tab[:, 12, :]
    scr[...] = jnp.zeros_like(scr)
    for t in range(STEPS):
        s = tab[:, t, :]
        use = BASE_USE + (use - BASE_USE) * USE_DECAY
        use = use + s * BASE_USE * (1.0 - use)
        release = s * use * supply
        supply = supply + SUPPLY_RATE * (1.0 - supply) - release
        fast = fast * PLUS_DECAY + s
        scr[:, t, :] = fast
        scr[:, STEPS + t, :] = release

    @pl.loop(0, ROWS, unroll=8)
    def _(g):
        terms = scr[g]
        high = terms.astype(BF16).astype(F32)
        low = terms - high
        qs[g] = jnp.concatenate([high[:20], low[:20], high[:20], jnp.zeros((4, G), F32)], axis=0).astype(BF16)
        driven = terms[STEPS : 2 * STEPS] * polarity
        dh = driven.astype(BF16).astype(F32)
        dl = driven - dh
        pad6 = jnp.zeros((6, G), F32)
        wide = jnp.concatenate([dh, pad6, dl, pad6, jnp.zeros((G - 32, G), F32)], axis=0)
        tall = jnp.transpose(wide)
        only = jnp.where(lane < 16, tall, 0.0)
        ds[g, pl.ds(0, G), :] = tall.astype(BF16)
        ds[g, pl.ds(G, G), :] = only.astype(BF16)

    for half, source in enumerate((rtab, ptab)):
        fast_p, slow_p = source[:, 13, :], source[:, 14, :]
        for t in range(STEPS):
            s = source[:, t, :]
            scr[pl.ds(half * COLS, COLS), t, :] = s * (PAIR_UP + TRIPLET_UP * slow_p)
            scr[pl.ds(half * COLS, COLS), STEPS + t, :] = -(PAIR_DOWN * fast_p)
            fast_p = fast_p * MINUS_DECAY + s
            slow_p = slow_p * SLOW_DECAY + s

    @pl.loop(0, 2 * COLS, unroll=8)
    def _(g):
        terms = scr[g] * LEARN_RATE
        high = terms.astype(BF16).astype(F32)
        low = terms - high
        rows = jnp.concatenate([high[:20], high[:20], low[:20], jnp.zeros((G - 60, G), F32)], axis=0)
        ps[g] = jnp.transpose(rows).astype(BF16)

    acc[...] = jnp.zeros_like(acc)

    @pl.loop(0, steps)
    def _(step):
        chunk = pl.ds(step * CHUNK, CHUNK)
        pltpu.make_async_copy(weights.at[pl.ds(0, CHUNK)], win.at[chunk], sem_in.at[step]).wait()
        currents = []
        for b in range(CHUNK):
            s = step * CHUNK + b
            moved, there = tables[6, s] >= 1, tables[7, s]
            p = jnp.where(moved, pidx[0, there], pre[s])
            q = jnp.where(moved, pidx[1, there] + COLS, post[s])
            w = win[s]
            change = jnp.dot(ps[q][:, :KP], qs[p], preferred_element_type=F32)
            wh, wl = split(w)
            currents.append((q, jnp.dot(jnp.concatenate([wh, wl], axis=1), ds[p], preferred_element_type=F32)))
            wout[s] = jnp.clip(w + change, 0.0, WEIGHT_MAX)
        for q, value in currents:
            acc[q] += value
        pltpu.make_async_copy(wout.at[chunk], new.at[chunk], sem_out).start()

    for q in range(2 * COLS):
        turned = jnp.transpose(acc[q])
        cur[q] = turned[0:16] + turned[16:32]
    pltpu.make_async_copy(wout, new, sem_out).wait()


def do_blocks(tables, pre, post, pidx, tab, rtab, ptab, weights, staged, z0):
    dma = pltpu.SemaphoreType.DMA
    return pl.pallas_call(
        blocks_kernel,
        out_shape=(jax.ShapeDtypeStruct((HALF, G, G), F32), jax.ShapeDtypeStruct((2 * COLS, 16, G), F32)),
        in_specs=[SMEM, SMEM, SMEM, SMEM, VMEM, VMEM, VMEM, ANY, ANY, ANY],
        out_specs=(ANY, VMEM),
        scratch_shapes=[
            pltpu.VMEM((ROWS, KP, G), BF16),
            pltpu.VMEM((ROWS, 2 * G, G), BF16),
            pltpu.VMEM((2 * COLS, G, G), BF16),
            pltpu.VMEM((ROWS, 24, G), F32),
            pltpu.VMEM((2 * COLS, G, G), F32),
            pltpu.VMEM((HALF, G, G), F32),
            pltpu.VMEM((HALF, G, G), F32),
            dma((HALF // CHUNK,)), dma,
        ],
        compiler_params=pltpu.CompilerParams(vmem_limit_bytes=VMEM_LIMIT),
        name="blocks",
    )(tables, pre, post, pidx, tab, rtab, ptab, weights, staged, z0)


def currents_kernel(cur, out, got, ss, rs):
    row, col = place()
    far = across(row)
    peers, copies, arrivals = [], [], []
    for d in range(1, COLS):
        c = lax.rem(col + d, COLS)
        peers.append(at(row, c))
        copies.append(send(cur.at[c], got.at[col], ss.at[d], rs.at[col], at(row, c)))
        arrivals.append(send(cur.at[c], got.at[c], ss.at[d], rs.at[c], at(row, c)))
    for d in range(COLS):
        c = lax.rem(col + d, COLS)
        peers.append(at(far, c))
        copies.append(send(cur.at[COLS + c], got.at[COLS + col], ss.at[COLS + d], rs.at[COLS + col], at(far, c)))
        arrivals.append(send(cur.at[COLS + c], got.at[COLS + c], ss.at[COLS + d], rs.at[COLS + c], at(far, c)))
    greet(peers)
    for copy in copies:
        copy.start()
    got[col] = cur[col]
    for copy in arrivals:
        copy.wait()
    drive = got[0]
    for i in range(1, 2 * COLS):
        drive = drive + got[i]
    gain = 1.0 / math.sqrt(G * HALF)
    state = jnp.zeros((1, G), F32)
    for t in range(STEPS):
        state = state * SYN_DECAY + gain * drive[t : t + 1]
        out[pl.ds(t, 1), :] = state


def settle(cur):
    dma = pltpu.SemaphoreType.DMA
    return pl.pallas_call(
        currents_kernel,
        out_shape=jax.ShapeDtypeStruct((STEPS, G), F32),
        in_specs=[VMEM],
        out_specs=VMEM,
        scratch_shapes=[pltpu.VMEM((2 * COLS, 16, G), F32), dma((2 * COLS,)), dma((2 * COLS,))],
        compiler_params=pltpu.CompilerParams(collective_id=1, has_side_effects=True),
        name="currents",
    )(cur)


def body(spikes, stp_init, trace_init, weights, block_pre, block_post, block_count):
    own = weights[0, 0]
    pre, post = block_pre[0, 0], block_post[0, 0]
    tab, rtab, ptab, pidx, tables, rung, z0, early = first(
        spikes, stp_init, trace_init, block_count, pre.reshape(2, G), post.reshape(2, G), own
    )
    staged = lax.switch(
        rung[0], [functools.partial(move, i) for i in range(len(RUNGS) + 1)], tables, own, early
    )
    new, cur = do_blocks(tables, pre, post, pidx, tab, rtab, ptab, own, staged, z0)
    synaptic = settle(cur)
    return (new[None, None], synaptic)


def solution(mesh):
    placed = (
        P(None, ("row", "col")),
        P(None, ("row", "col")),
        P(None, ("row", "col")),
        P("row", "col", None, None, None),
        P("row", "col", None),
        P("row", "col", None),
        P("row", "col"),
    )
    return jax.shard_map(
        body,
        mesh=mesh,
        in_specs=placed,
        out_specs=(P("row", "col", None, None, None), P(None, ("row", "col"))),
        check_vma=False,
    )
```

profile of v0, /device:TPU:0, one launch (start us, length us, event | category | flops | bytes accessed | tf_op | source)
XLA Modules:
  0.0 118.0 jit_solution(3246422978073085990)
XLA Ops:
  1.3 37.7 %first.1 = (f32[32,16,128]{2,1,0:T(8,128)}, f32[4,16,128]{2,1,0:T(8,128)}, f32[4,16,128]{2,1,0:T(8,128)}, s32[8,128]{1,0:T(8,128)}, s32[8,128]{1,0:T(8,128)S(1)}...) custom-call(s32[10,128]{1,0:T(8,128)} %spikes.1, f32[2,128]{1,0:T(2,128)} %stp.1, f32[3,128]{1,0:T(4,128)} %trace.1, ...), custom_call_target="tpu_custom_call" | custom-call | tf_op jit(solution)/shard_map/first/pallas_call | solution.py:221
  39.6 55.8 %conditional.1 = (f32[216,128,128]{2,1,0:T(8,128)}) conditional(s32[]{:T(128)} %bitcast.5, (s32[8,128]{1,0:T(8,128)S(1)}, f32[256,128,128]{2,1,0:T(8,128)}, f32[88,128,128]{2,1,0:T(8,128)}) %tuple.32, (s32[8,128]{1,0:T(8,128)S(1)}, f32[256,128,128]{2,1,0:T(8,128)}, f32[88,128,128]{2,1,0:T(8,128)}) %tuple.33, ...), branch_computations={%region_0.0_spmd, %region_1.0_spmd, %region_2.0_spmd, %region_3.0_... | conditional | bytes 8 | solution.py:683
  39.7 55.8 %move_32.1 = f32[216,128,128]{2,1,0:T(8,128)} custom-call(s32[8,128]{1,0:T(8,128)S(1)} %get-tuple-element.34.tables, f32[256,128,128]{2,1,0:T(8,128)} %get-tuple-element.35.weights, f32[88,128,128]{2,1,0:T(8,128)} %get-tuple-element.36.early), custom_call_target="tpu_custom_call" | custom-call | tf_op jit(solution)/shard_map/cond/branch_1_fun/move_32/pallas_call | solution.py:490
  95.5 11.7 %blocks.1 = (f32[128,128,128]{2,1,0:T(8,128)}, f32[8,16,128]{2,1,0:T(8,128)}) custom-call(s32[8,128]{1,0:T(8,128)S(1)} %get-tuple-element.55.tables, s32[256]{0:T(256)} %bitcast.15, s32[256]{0:T(256)} %bitcast.17, s32[8,128]{1,0:T(8,128)} %get-tuple-element.56.pidx, f32[32,16,128]{2,1,0:T(8,128)} %get-tuple-element.57.tab, ...), custom_call_target="tpu_custom_call" | custom-call | tf_op jit(solution)/shard_map/blocks/pallas_call | solution.py:614
  107.1 9.5 %currents.1 = f32[10,128]{1,0:T(8,128)} custom-call(f32[8,16,128]{2,1,0:T(8,128)} %get-tuple-element.64.cur), custom_call_target="tpu_custom_call" | custom-call | tf_op jit(solution)/shard_map/currents/pallas_call | solution.py:666
  116.7 1.3 %copy.16 = f32[10,128]{1,0:T(8,128)} copy(f32[10,128]{1,0:T(8,128)} %currents.1) | data formatting | bytes 10240
where the time goes:
time: 118 us
  Pallas kernels  115 us (97%)
  between operations  2 us (2%)
  local copies, waits for them, and re-layouts  1.3 us (1%)
    pallas_call x1, Pallas kernels, move(): pl.pallas_call(functools.partial(move_kernel, ends), out_shape=STAGED, in...  55.8 us
    pallas_call x1, Pallas kernels, first(): pl.pallas_call(first_kernel, out_shape=(jax.ShapeDtypeStruct((ROWS, 16, G...  37.7 us
    pallas_call x1, Pallas kernels, do_blocks(): pl.pallas_call(blocks_kernel, out_shape=(jax.ShapeDtypeStruct((HALF, G, G...  11.7 us
    pallas_call x1, Pallas kernels, settle(): pl.pallas_call(currents_kernel, out_shape=jax.ShapeDtypeStruct((STEPS, G)...  9.51 us

commit v1 on v0

--- a/solution.py
+++ b/solution.py
@@ -503,7 +503,7 @@
     )(tables, weights, early)
 
 
-CHUNK = 8
+CHUNK = 16
 KP = 64
 
 
@@ -549,7 +549,7 @@
         scr[:, t, :] = fast
         scr[:, STEPS + t, :] = release
 
-    @pl.loop(0, ROWS, unroll=8)
+    @pl.loop(0, ROWS, unroll=16)
     def _(g):
         terms = scr[g]
         high = terms.astype(BF16).astype(F32)

time: 118 us -> 119 us (level); the launches traced: 118 us -> 117 us
  Pallas kernels: 115 us -> 113 us
    pallas_call x1, Pallas kernels: 11.7 us -> 10.3 us  [do_blocks(): pl.pallas_call(blocks_kernel, out_shape=(jax.ShapeDtypeStruct((HALF, G, G...]
where the time goes in v1:
time: 119 us; the launch traced here: 117 us
  Pallas kernels  113 us (95%)
  between operations  2 us (2%)
  local copies, waits for them, and re-layouts  1.3 us (1%)
    pallas_call x1, Pallas kernels, move(): pl.pallas_call(functools.partial(move_kernel, ends), out_shape=STAGED, in...  55.8 us
    pallas_call x1, Pallas kernels, first(): pl.pallas_call(first_kernel, out_shape=(jax.ShapeDtypeStruct((ROWS, 16, G...  37.7 us
    pallas_call x1, Pallas kernels, do_blocks(): pl.pallas_call(blocks_kernel, out_shape=(jax.ShapeDtypeStruct((HALF, G, G...  10.3 us
    pallas_call x1, Pallas kernels, settle(): pl.pallas_call(currents_kernel, out_shape=jax.ShapeDtypeStruct((STEPS, G)...  9.51 us

profile of v1, /device:TPU:0, one launch (start us, length us, event | category | flops | bytes accessed | tf_op | source)
XLA Modules:
  0.0 116.6 jit_solution(9846457400696370163)
XLA Ops:
  1.3 37.7 %first.1 = (f32[32,16,128]{2,1,0:T(8,128)}, f32[4,16,128]{2,1,0:T(8,128)}, f32[4,16,128]{2,1,0:T(8,128)}, s32[8,128]{1,0:T(8,128)}, s32[8,128]{1,0:T(8,128)S(1)}...) custom-call(s32[10,128]{1,0:T(8,128)} %spikes.1, f32[2,128]{1,0:T(2,128)} %stp.1, f32[3,128]{1,0:T(4,128)} %trace.1, ...), custom_call_target="tpu_custom_call" | custom-call | tf_op jit(solution)/shard_map/first/pallas_call | solution.py:221
  39.6 55.8 %conditional.1 = (f32[216,128,128]{2,1,0:T(8,128)}) conditional(s32[]{:T(128)} %bitcast.5, (s32[8,128]{1,0:T(8,128)S(1)}, f32[256,128,128]{2,1,0:T(8,128)}, f32[88,128,128]{2,1,0:T(8,128)}) %tuple.32, (s32[8,128]{1,0:T(8,128)S(1)}, f32[256,128,128]{2,1,0:T(8,128)}, f32[88,128,128]{2,1,0:T(8,128)}) %tuple.33, ...), branch_computations={%region_0.0_spmd, %region_1.0_spmd, %region_2.0_spmd, %region_3.0_... | conditional | bytes 8 | solution.py:683
  39.7 55.8 %move_32.1 = f32[216,128,128]{2,1,0:T(8,128)} custom-call(s32[8,128]{1,0:T(8,128)S(1)} %get-tuple-element.34.tables, f32[256,128,128]{2,1,0:T(8,128)} %get-tuple-element.35.weights, f32[88,128,128]{2,1,0:T(8,128)} %get-tuple-element.36.early), custom_call_target="tpu_custom_call" | custom-call | tf_op jit(solution)/shard_map/cond/branch_1_fun/move_32/pallas_call | solution.py:490
  95.5 10.3 %blocks.1 = (f32[128,128,128]{2,1,0:T(8,128)}, f32[8,16,128]{2,1,0:T(8,128)}) custom-call(s32[8,128]{1,0:T(8,128)S(1)} %get-tuple-element.55.tables, s32[256]{0:T(256)} %bitcast.15, s32[256]{0:T(256)} %bitcast.17, s32[8,128]{1,0:T(8,128)} %get-tuple-element.56.pidx, f32[32,16,128]{2,1,0:T(8,128)} %get-tuple-element.57.tab, ...), custom_call_target="tpu_custom_call" | custom-call | tf_op jit(solution)/shard_map/blocks/pallas_call | solution.py:614
  105.8 9.5 %currents.1 = f32[10,128]{1,0:T(8,128)} custom-call(f32[8,16,128]{2,1,0:T(8,128)} %get-tuple-element.64.cur), custom_call_target="tpu_custom_call" | custom-call | tf_op jit(solution)/shard_map/currents/pallas_call | solution.py:666
  115.3 1.3 %copy.16 = f32[10,128]{1,0:T(8,128)} copy(f32[10,128]{1,0:T(8,128)} %currents.1) | data formatting | bytes 10240
